TPU v7x, 32 devices: a whole 2x2x4 slice. The times are simulated.
32 devices in a mesh: gx: 4 (over y, x), gy: 8 (over z, core).
Axes of the slice: x: 2, y: 2, z: 4, core: 2. Of those that a mesh axis runs over, the one named last changes fastest.
Arguments:
- species_means: bfloat16 [8, 16, 120, 512], P(None, 'gy', None, 'gx'), may hold values from 0.19921875 to 5
- zonal_edge_velocity: float32 [16, 120, 512], P('gy', None, 'gx'), may hold values from -6 to 6
- meridional_edge_velocity: float32 [16, 120, 512], P('gy', None, 'gx'), may hold values from -6 to 6
- scaled_warmth: float32 [16, 120, 512], P('gy', None, 'gx'), may hold values from 0.5 to 2
- donor_depths: float32 [16, 120, 512], P('gy', None, 'gx'), may hold values from 0.5 to 2
- leading_donor_level: int32 [16, 120, 512], P('gy', None, 'gx'), may hold values from 0 to 118, as said below
- opening_share: bfloat16 [16, 120, 512], P('gy', None, 'gx'), may hold values from 0 to 0.44921875
- closing_share: bfloat16 [16, 120, 512], P('gy', None, 'gx'), may hold values from 0.546875 to 1
Outputs:
- tracers_out: float32 [8, 16, 120, 512], P(None, 'gy', None, 'gx')
- regridded_zonal: float32 [16, 120, 512], P('gy', None, 'gx')
- regridded_meridional: float32 [16, 120, 512], P('gy', None, 'gx')
- adjusted_warmth: float32 [16, 120, 512], P('gy', None, 'gx')
Inputs may be any that keep to these rules, and one draw needn't show every extreme that they name: Target layer k draws on source layers leading_donor_level and leading_donor_level + 1, and leading_donor_level lies within 2 of k.
All inputs are finite; a program needn't handle non-finite values.
Results may differ from a plain program's by a relative error of at most 0.0003.
Values sent between devices are 32-bit elements; how exact they have to be, the bound alone decides.
A program may use at most 64 MiB of HBM per device.

v0:
```python
import jax
import jax.numpy as jnp
from jax import lax
from jax.sharding import PartitionSpec as P

thermal_rescale_factor = 3.5
offsets_all = (-2, -1, 0, 1, 2, 3)


def passed_along(value, axis, steps):
    count = lax.axis_size(axis)
    pairs = [(source, (source + steps) % count) for source in range(count)]
    return lax.ppermute(value, axis, pairs)


def ppm_parts(values):
    layers = values.shape[-2]
    top_edge = 1.5 * values[..., 0:1, :] - 0.5 * values[..., 1:2, :]
    second_edge = 0.5 * (values[..., 0:1, :] + values[..., 1:2, :])
    inner_edge = 7.0 / 12.0 * (
        values[..., 1 : layers - 2, :] + values[..., 2 : layers - 1, :]
    ) - 1.0 / 12.0 * (values[..., 0 : layers - 3, :] + values[..., 3:layers, :])
    lower_edge = 0.5 * (
        values[..., layers - 2 : layers - 1, :] + values[..., layers - 1 : layers, :]
    )
    bottom_edge = (
        1.5 * values[..., layers - 1 : layers, :] - 0.5 * values[..., layers - 2 : layers - 1, :]
    )
    edge_values = jnp.concatenate(
        [top_edge, second_edge, inner_edge, lower_edge, bottom_edge], axis=-2
    )
    left_edge = edge_values[..., :layers, :]
    right_edge = edge_values[..., 1:, :]
    return (left_edge, right_edge - left_edge, 6.0 * values - 3.0 * (left_edge + right_edge))


def shifted_layers(values, amount):
    layers = values.shape[-2]
    if amount == 0:
        return values
    if amount > 0:
        filler = jnp.zeros(values.shape[:-2] + (amount, values.shape[-1]), values.dtype)
        return jnp.concatenate([values[..., amount:, :], filler], axis=-2)
    filler = jnp.zeros(values.shape[:-2] + (-amount, values.shape[-1]), values.dtype)
    return jnp.concatenate([filler, values[..., : layers + amount, :]], axis=-2)


def pick_layers(values, masks):
    total = jnp.zeros(values.shape, jnp.float32)
    for amount, selector in zip(offsets_all, masks):
        total = total + jnp.where(selector, shifted_layers(values, amount), 0.0)
    return total


def build_operator(donor_depths, leading_donor_level, opening_share, closing_share):
    start_frac = opening_share.astype(jnp.float32)
    end_frac = closing_share.astype(jnp.float32)
    layer_offset = leading_donor_level - lax.broadcasted_iota(
        jnp.int32, leading_donor_level.shape, 1
    )
    first_masks = [layer_offset == amount for amount in offsets_all]
    second_masks = [layer_offset + 1 == amount for amount in offsets_all]
    weight_first = (1.0 - start_frac) * pick_layers(donor_depths, first_masks)
    weight_second = end_frac * pick_layers(donor_depths, second_masks)
    linear_first = 0.5 * (start_frac + 1.0)
    square_first = linear_first - (start_frac * start_frac + start_frac + 1.0) / 3.0
    linear_second = 0.5 * end_frac
    square_second = linear_second - end_frac * end_frac / 3.0
    return (
        first_masks,
        second_masks,
        weight_first,
        weight_second,
        linear_first,
        square_first,
        linear_second,
        square_second,
    )


def multiply_by_regrid_operator(operator, values):
    (
        first_masks,
        second_masks,
        weight_first,
        weight_second,
        linear_first,
        square_first,
        linear_second,
        square_second,
    ) = operator
    left_edge, edge_slope, curvature = ppm_parts(values)
    mean_first = (
        pick_layers(left_edge, first_masks)
        + pick_layers(edge_slope, first_masks) * linear_first
        + pick_layers(curvature, first_masks) * square_first
    )
    mean_second = (
        pick_layers(left_edge, second_masks)
        + pick_layers(edge_slope, second_masks) * linear_second
        + pick_layers(curvature, second_masks) * square_second
    )
    return (weight_first * mean_first + weight_second * mean_second) / (
        weight_first + weight_second
    )


def local(
    species_means,
    zonal_edge_velocity,
    meridional_edge_velocity,
    scaled_warmth,
    donor_depths,
    leading_donor_level,
    opening_share,
    closing_share,
):
    vertical_regrid_operator = build_operator(
        donor_depths, leading_donor_level, opening_share, closing_share
    )
    regridded_depths = vertical_regrid_operator[2] + vertical_regrid_operator[3]
    mass_before = jnp.sum(species_means.astype(jnp.float32) * donor_depths, axis=(1, 2, 3))
    interior_u_faces = 0.5 * jnp.sum(
        0.5
        * (donor_depths[:-1] + donor_depths[1:])
        * zonal_edge_velocity[:-1]
        * zonal_edge_velocity[:-1]
    )
    interior_v_faces = 0.5 * jnp.sum(
        0.5
        * (donor_depths[:, :, :-1] + donor_depths[:, :, 1:])
        * meridional_edge_velocity[:, :, :-1]
        * meridional_edge_velocity[:, :, :-1]
    )
    local_prior_totals = (
        thermal_rescale_factor * jnp.sum(donor_depths * scaled_warmth)
        + interior_u_faces
        + interior_v_faces
    )
    from_south = passed_along(zonal_edge_velocity[-1:], "gy", 1)
    u_paired = multiply_by_regrid_operator(
        vertical_regrid_operator,
        jnp.stack(
            [zonal_edge_velocity, jnp.concatenate([from_south, zonal_edge_velocity[:-1]], axis=0)]
        ),
    )
    u_cross = u_paired[1]
    returned = passed_along(
        jnp.stack([u_cross[0:1], donor_depths[0:1], regridded_depths[0:1]]), "gy", -1
    )
    north_thick = returned[2]
    edge_u = 0.5 * jnp.sum(
        0.5
        * (donor_depths[-1:] + returned[1])
        * zonal_edge_velocity[-1:]
        * zonal_edge_velocity[-1:]
    )
    regridded_zonal = 0.5 * (u_paired[0] + jnp.concatenate([u_cross[1:], returned[0]], axis=0))
    zonal_following = 0.5 * jnp.sum(
        0.5
        * (regridded_depths + jnp.concatenate([regridded_depths[1:], north_thick], axis=0))
        * regridded_zonal
        * regridded_zonal
    )
    from_west = passed_along(meridional_edge_velocity[:, :, -1:], "gx", 1)
    v_paired = multiply_by_regrid_operator(
        vertical_regrid_operator,
        jnp.stack(
            [
                meridional_edge_velocity,
                jnp.concatenate([from_west, meridional_edge_velocity[:, :, :-1]], axis=2),
            ]
        ),
    )
    v_cross = v_paired[1]
    v_returned = passed_along(
        jnp.stack([v_cross[:, :, 0:1], donor_depths[:, :, 0:1], regridded_depths[:, :, 0:1]]),
        "gx",
        -1,
    )
    regridded_meridional = 0.5 * (
        v_paired[0] + jnp.concatenate([v_cross[:, :, 1:], v_returned[0]], axis=2)
    )
    edge_v = 0.5 * jnp.sum(
        0.5
        * (donor_depths[:, :, -1:] + v_returned[1])
        * meridional_edge_velocity[:, :, -1:]
        * meridional_edge_velocity[:, :, -1:]
    )
    meridional_following = 0.5 * jnp.sum(
        0.5
        * (regridded_depths + jnp.concatenate([regridded_depths[:, :, 1:], v_returned[2]], axis=2))
        * regridded_meridional
        * regridded_meridional
    )
    tracer_new = multiply_by_regrid_operator(
        vertical_regrid_operator, species_means.astype(jnp.float32)
    )
    regridded_warmth = multiply_by_regrid_operator(vertical_regrid_operator, scaled_warmth)
    mass_after = jnp.sum(tracer_new * regridded_depths, axis=(1, 2, 3))
    aggregate_regridded = jnp.sum(regridded_depths)
    kinetic_thermal_following = (
        thermal_rescale_factor * jnp.sum(regridded_depths * regridded_warmth)
        + zonal_following
        + meridional_following
    )
    mass_total_before, mass_total_after, scalars = lax.psum(
        (
            mass_before,
            mass_after,
            jnp.stack(
                [
                    local_prior_totals + edge_u + edge_v,
                    kinetic_thermal_following,
                    aggregate_regridded,
                ]
            ),
        ),
        ("gx", "gy"),
    )
    enthalpy_global_preceding = scalars[0]
    enthalpy_global_following = scalars[1]
    thick_total = scalars[2]
    tracers_out = (
        tracer_new + ((mass_total_before - mass_total_after) / thick_total)[:, None, None, None]
    )
    adjusted_warmth = regridded_warmth + (enthalpy_global_preceding - enthalpy_global_following) / (
        thermal_rescale_factor * thick_total
    )
    return (tracers_out, regridded_zonal, regridded_meridional, adjusted_warmth)


def solution(mesh):
    in_specs = (
        P(None, "gy", None, "gx"),
        P("gy", None, "gx"),
        P("gy", None, "gx"),
        P("gy", None, "gx"),
        P("gy", None, "gx"),
        P("gy", None, "gx"),
        P("gy", None, "gx"),
        P("gy", None, "gx"),
    )
    out_specs = (
        P(None, "gy", None, "gx"),
        P("gy", None, "gx"),
        P("gy", None, "gx"),
        P("gy", None, "gx"),
    )
    return jax.shard_map(local, mesh=mesh, in_specs=in_specs, out_specs=out_specs, check_vma=False)
```

profile of v0, /device:TPU:0, one launch (start us, length us, event | category | flops | bytes accessed | tf_op | source)
XLA Modules:
  0.0 95.7 jit_solution(4133730569461327342)
XLA Ops:
  0.6 1.7 %slice.551 = f32[2,120,1]{2,1,0:T(8,128)} slice(f32[2,120,128]{2,1,0:T(8,128)} %param.10), slice={[0:2], [0:120], [127:128]} | slice | bytes 1920 | tf_op jit(solution)/shard_map/slice | solution.py:165
  2.3 3.0 %collective-permute-start.2 = (f32[2,120,1]{2,1,0:T(8,128)}, f32[2,120,1]{2,1,0:T(8,128)S(1)}, u32[]{:S(2)}, u32[]{:S(2)}) collective-permute-start(f32[2,120,1]{2,1,0:T(8,128)} %slice.551), channel_id=1, source_target_pairs={{0,8},{8,16},{16,24},{24,0},{1,9},{9,17},{17,25},{25,1},{2,10},{10... | collective-permute-start | bytes 2888 | tf_op jit(solution)/shard_map/ppermute | solution.py:13
  6.0 1.0 %copy-done.2 = bf16[8,2,120,128]{3,2,1,0:T(8,128)(2,1)S(1)} copy-done((bf16[8,2,120,128]{3,2,1,0:T(8,128)(2,1)S(1)}, bf16[8,2,120,128]{3,2,1,0:T(8,128)(2,1)}, u32[]{:S(2)}) %copy-start.2) | copy-done | bytes 491544
  9.2 0.8 copy-done.1
  10.0 0.8 fusion.46
  11.5 0.7 fusion.102
  12.6 0.7 fusion.61
  13.3 0.8 fusion.98
  14.1 0.8 fusion.99
  14.9 0.7 fusion.40
  15.5 0.7 pad_maximum_fusion.20
  16.2 7.7 %multiply_reduce_fusion = (f32[8]{0:T(128)S(1)}, f32[8,2,120,128]{3,2,1,0:T(8,128)S(1)}) fusion(f32[2,120,128]{2,1,0:T(8,128)S(1)} %get-tuple-element.125, f32[2,120,128]{2,1,0:T(8,128)S(1)} %get-tuple-element.141, f32[2,120,128]{2,1,0:T(8,128)S(1)} %get-tuple-element.140, pred[2,120,128]{2,1,0:T(8,128)(4,1)S(1)} %get-tuple-element.127, ...), kind=kLoop, calls=%fused_computation.18 | loop fusion | flops 24084472 | bytes 17244192 | tf_op jit(solution)/shard_map/reduce_sum | solution.py:200
  24.0 0.8 slice.715
  24.7 0.7 slice.709
  25.4 0.7 slice.704
  28.1 1.0 %add_divide_fusion.1 = f32[2,2,120,128]{3,2,1,0:T(8,128)S(1)} fusion(f32[2,2,120,128]{3,2,1,0:T(8,128)S(1)} %get-tuple-element.71, f32[2,2,117,128]{3,2,1,0:T(8,128)S(1)} %slice.692, f32[2,2,118,128]{3,2,1,0:T(8,128)S(1)} %get-tuple-element.90, f32[2,2,119,128]{3,2,1,0:T(8,128)S(1)} %get-tuple-element.92, f32[2,2,119,128]{3,2,1,0:T(8,128)S(1)} %get-tuple-element.91, ...), kind=kLoop, calls=%fused_computation.105 | loop fusion | flops 5591040 | bytes 5355520 | tf_op jit(solution)/shard_map/div | solution.py:103
  29.2 0.7 slice.718
  29.9 1.2 %collective-permute-start.3 = (f32[3,2,120,1]{2,1,3,0:T(2,128)S(1)}, f32[3,2,120,1]{2,1,3,0:T(2,128)S(1)}, u32[]{:S(2)}, u32[]{:S(2)}) collective-permute-start(f32[3,2,120,1]{2,1,3,0:T(2,128)S(1)} %pad_maximum_fusion.23), channel_id=1, source_target_pairs={{0,24},{8,0},{16,8},{24,16},{1,25},{9,1},{17,9},{25,17},{2,26},{10... | collective-permute-start | bytes 8648 | tf_op jit(solution)/shard_map/ppermute | solution.py:13
  31.1 0.8 maximum_bitcast_fusion
  32.6 1.0 %add_divide_fusion.2 = f32[2,2,120,128]{3,2,1,0:T(8,128)S(1)} fusion(f32[2,2,120,128]{3,2,1,0:T(8,128)S(1)} %get-tuple-element.69, f32[2,2,117,128]{3,2,1,0:T(8,128)S(1)} %slice.660, f32[2,2,118,128]{3,2,1,0:T(8,128)S(1)} %get-tuple-element.79, f32[2,2,119,128]{3,2,1,0:T(8,128)S(1)} %get-tuple-element.81, f32[2,2,119,128]{3,2,1,0:T(8,128)S(1)} %get-tuple-element.80, ...), kind=kLoop, calls=%fused_computation.106 | loop fusion | flops 5591040 | bytes 5355520 | tf_op jit(solution)/shard_map/div | solution.py:103
  34.4 0.7 pad_maximum_fusion.17
  35.1 3.0 %collective-permute-start.1 = (f32[3,1,120,128]{3,2,1,0:T(8,128)}, f32[3,1,120,128]{3,2,1,0:T(8,128)}, u32[]{:S(2)}, u32[]{:S(2)}) collective-permute-start(f32[3,1,120,128]{3,2,1,0:T(8,128)} %pad_maximum_fusion.17), channel_id=1, source_target_pairs={{0,7},{1,0},{2,1},{3,2},{4,3},{5,4},{6,5},{7,6},{8,15},{9,8},{10,9... | collective-permute-start | bytes 552968 | tf_op jit(solution)/shard_map/ppermute | solution.py:13
  38.1 0.8 copy.187
  38.9 0.8 copy.188
  39.8 0.8 fusion.47
  41.4 0.9 slice_bitcast_fusion.3
  42.4 3.6 %fusion.49 = (f32[]{:T(128)}, f32[]{:T(128)}, f32[]{:T(128)}, f32[]{:T(128)}, f32[2,120,128]{2,1,0:T(8,128)}, /*index=5*/f32[2,120,128]{2,1,0:T(8,128)}, f32[2,120,128]{2,1,0:T(8,128)}) fusion(f32[2,120,128]{2,1,0:T(8,128)S(1)} %get-tuple-element.125, f32[2,120,1]{2,1,0:T(8,128)} %copy.187, f32[2,120,127]{2,1,0:T(8,128)} %slice.715, ...), kind=kLoop, calls=%fused_computation.136 | loop fusion | flops 3839996 | bytes 3906576 | tf_op jit(solution)/shard_map/reduce_sum | solution.py:190
  47.9 1.5 %fusion.63 = (f32[]{:T(128)}, f32[]{:T(128)}) fusion(f32[3,1,120,128]{3,2,1,0:T(8,128)} %collective-permute-done.1, f32[2,120,128]{2,1,0:T(8,128)S(1)} %copy-done, f32[2,120,128]{2,1,0:T(8,128)S(1)} %copy-done.4), kind=kLoop, calls=%fused_computation.176 | loop fusion | flops 153598 | bytes 307208 | tf_op jit(solution)/shard_map/reduce_sum | solution.py:152
  51.3 39.4 %all-reduce.65 = (f32[8]{0:T(128)S(1)}, f32[8]{0:T(128)S(1)}, f32[3]{0:T(128)S(1)}) all-reduce(f32[8]{0:T(128)S(1)} %get-tuple-element.67, f32[8]{0:T(128)S(1)} %get-tuple-element.36, f32[3]{0:T(128)S(1)} %pad_maximum_fusion.24), channel_id=1, replica_groups=mesh['gx'=4,'gy'=8] {'gx','gy'}, use_global_device_ids=true, to_apply=%region_1.2 | all-reduce | flops 19 | bytes 152 | tf_op jit(solution)/shard_map/psum | solution.py:207
  92.0 0.7 subtract_divide_fusion
  92.7 1.1 %broadcast_add_fusion = f32[8,2,120,128]{3,2,1,0:T(8,128)} fusion(f32[8,2,120,128]{3,2,1,0:T(8,128)S(1)} %get-tuple-element.37, f32[8]{0:T(128)S(1)} %subtract_divide_fusion), kind=kLoop, calls=%fused_computation.57 | loop fusion | flops 245760 | bytes 1966112 | tf_op jit(solution)/shard_map/add | solution.py:225
  95.1 0.7 broadcast_add_fusion.1
  (94 shorter events, 7.5 us)
Async XLA Ops:
  0.6 4.7 %copy-start.4 = (f32[2,120,128]{2,1,0:T(8,128)S(1)}, f32[2,120,128]{2,1,0:T(8,128)}, u32[]{:S(2)}) copy-start(f32[2,120,128]{2,1,0:T(8,128)} %param.9) | copy-start | bytes 368644
  2.3 3.6 %copy-start = (f32[2,120,128]{2,1,0:T(8,128)S(1)}, f32[2,120,128]{2,1,0:T(8,128)}, u32[]{:S(2)}) copy-start(f32[2,120,128]{2,1,0:T(8,128)} %param.12) | copy-start | bytes 368644
  2.3 25.1 %collective-permute-start.2 = (f32[2,120,1]{2,1,0:T(8,128)}, f32[2,120,1]{2,1,0:T(8,128)S(1)}, u32[]{:S(2)}, u32[]{:S(2)}) collective-permute-start(f32[2,120,1]{2,1,0:T(8,128)} %slice.551), channel_id=1, source_target_pairs={{0,8},{8,16},{16,24},{24,0},{1,9},{9,17},{17,25},{25,1},{2,10},{10... | collective-permute-start | bytes 2888 | tf_op jit(solution)/shard_map/ppermute | solution.py:13
  5.9 25.2 %collective-permute-start = (f32[1,120,128]{2,1,0:T(8,128)}, f32[1,120,128]{2,1,0:T(8,128)}, u32[]{:S(2)}, u32[]{:S(2)}) collective-permute-start(f32[1,120,128]{2,1,0:T(8,128)} %get-tuple-element.117), channel_id=1, source_target_pairs={{0,1},{1,2},{2,3},{3,4},{4,5},{5,6},{6,7},{7,0},{8,9},{9,10},{10,1... | collective-permute-start | bytes 184328 | tf_op jit(solution)/shard_map/ppermute | solution.py:13
  6.0 1.0 %copy-start.2 = (bf16[8,2,120,128]{3,2,1,0:T(8,128)(2,1)S(1)}, bf16[8,2,120,128]{3,2,1,0:T(8,128)(2,1)}, u32[]{:S(2)}) copy-start(bf16[8,2,120,128]{3,2,1,0:T(8,128)(2,1)} %param.8) | copy-start | bytes 1474564
  9.1 0.9 copy-start.1
  10.0 0.8 copy-start.12
  10.0 0.9 copy-start.13
  10.0 1.0 %copy-start.15 = (s32[2,120,128]{2,1,0:T(8,128)S(1)}, s32[2,120,128]{2,1,0:T(8,128)}, u32[]{:S(2)}) copy-start(s32[2,120,128]{2,1,0:T(8,128)} %param.13) | copy-start | bytes 368644
  11.5 1.0 copy-start.3
  29.9 8.1 %collective-permute-start.3 = (f32[3,2,120,1]{2,1,3,0:T(2,128)S(1)}, f32[3,2,120,1]{2,1,3,0:T(2,128)S(1)}, u32[]{:S(2)}, u32[]{:S(2)}) collective-permute-start(f32[3,2,120,1]{2,1,3,0:T(2,128)S(1)} %pad_maximum_fusion.23), channel_id=1, source_target_pairs={{0,24},{8,0},{16,8},{24,16},{1,25},{9,1},{17,9},{25,17},{2,26},{10... | collective-permute-start | bytes 8648 | tf_op jit(solution)/shard_map/ppermute | solution.py:13
  33.5 0.8 copy-start.11
  35.1 6.4 %collective-permute-start.1 = (f32[3,1,120,128]{3,2,1,0:T(8,128)}, f32[3,1,120,128]{3,2,1,0:T(8,128)}, u32[]{:S(2)}, u32[]{:S(2)}) collective-permute-start(f32[3,1,120,128]{3,2,1,0:T(8,128)} %pad_maximum_fusion.17), channel_id=1, source_target_pairs={{0,7},{1,0},{2,1},{3,2},{4,3},{5,4},{6,5},{7,6},{8,15},{9,8},{10,9... | collective-permute-start | bytes 552968 | tf_op jit(solution)/shard_map/ppermute | solution.py:13
  38.9 3.4 %copy-start.7 = (f32[2,118,128]{2,1,0:T(8,128)S(1)}, f32[2,118,128]{2,1,0:T(8,128)}, u32[]{:S(2)}) copy-start(f32[2,118,128]{2,1,0:T(8,128)} %get-tuple-element.156) | copy-start | bytes 362500
  38.9 3.5 %copy-start.8 = (f32[2,118,128]{2,1,0:T(8,128)S(1)}, f32[2,118,128]{2,1,0:T(8,128)}, u32[]{:S(2)}) copy-start(f32[2,118,128]{2,1,0:T(8,128)} %get-tuple-element.157) | copy-start | bytes 362500
  38.9 3.5 %copy-start.14 = (f32[1,120,128]{2,1,0:T(8,128)S(1)}, f32[1,120,128]{2,1,0:T(8,128)}, u32[]{:S(2)}) copy-start(f32[1,120,128]{2,1,0:T(8,128)} %get-tuple-element.115) | copy-start | bytes 184324
  39.6 2.7 %copy-start.9 = (f32[2,119,128]{2,1,0:T(8,128)S(1)}, f32[2,119,128]{2,1,0:T(8,128)}, u32[]{:S(2)}) copy-start(f32[2,119,128]{2,1,0:T(8,128)} %get-tuple-element.109) | copy-start | bytes 365572
  41.3 1.1 %copy-start.5 = (f32[2,118,128]{2,1,0:T(8,128)S(1)}, f32[2,118,128]{2,1,0:T(8,128)}, u32[]{:S(2)}) copy-start(f32[2,118,128]{2,1,0:T(8,128)} %get-tuple-element.107) | copy-start | bytes 362500
  41.3 1.1 %copy-start.6 = (f32[2,118,128]{2,1,0:T(8,128)S(1)}, f32[2,118,128]{2,1,0:T(8,128)}, u32[]{:S(2)}) copy-start(f32[2,118,128]{2,1,0:T(8,128)} %get-tuple-element.108) | copy-start | bytes 362500
  92.6 2.4 %copy-start.10 = (f32[2,120,128]{2,1,0:T(8,128)S(1)}, f32[2,120,128]{2,1,0:T(8,128)}, u32[]{:S(2)}) copy-start(f32[2,120,128]{2,1,0:T(8,128)} %get-tuple-element.21) | copy-start | bytes 368644
where the time goes:
time: 96.3 us; the launch traced here: 95.7 us
  blocking collectives  39.4 us (41%)
  other arithmetic  25.4 us (26%)
  local copies, waits for them, and re-layouts  15.2 us (16%)
  between operations  8.29 us (9%)
  starting transfers between devices  7.19 us (7%)
    psum x1, blocking collectives, local(): lax.psum((mass_before, mass_after, jnp.stack([local_prior_totals + edge_u...  39.4 us
    reduce_sum x1, other arithmetic, local(): mass_after = jnp.sum(tracer_new * regridded_depths, axis=(1, 2, 3))  7.73 us
    ppermute x4, starting transfers between devices, passed_along(): return lax.ppermute(value, axis, pairs)  7.19 us
    reduce_sum x1, other arithmetic, local(): jnp.sum(0.5 * (regridded_depths + jnp.concatenate([regridded_depths[:, :,...  3.62 us
    slice x14, local copies, waits for them, and re-layouts, shifted_layers(): return jnp.concatenate([filler, values[..., :layers + amount, :]], axis=-2)  2.64 us
    unnamed x33, local copies, waits for them, and re-layouts  2.56 us
    div x2, other arithmetic, multiply_by_regrid_operator(): (weight_first * mean_first + weight_second * mean_second) / (weight_first...  1.98 us
  transfers between devices with their start and end apart: 4, of which 1 were waited for; matrix products, arithmetic and copies ran while one was open for 28% of the time, Pallas kernels for 0%

commit v1 on v0

--- a/solution.py
+++ b/solution.py
@@ -115,6 +115,10 @@
     opening_share,
     closing_share,
 ):
+
+    def perform_numbers(block_in):
+        return lax.psum(lax.psum(block_in, "gx"), axis_name="gy")
+
     vertical_regrid_operator = build_operator(
         donor_depths, leading_donor_level, opening_share, closing_share
     )
@@ -204,7 +208,7 @@
         + zonal_following
         + meridional_following
     )
-    mass_total_before, mass_total_after, scalars = lax.psum(
+    mass_total_before, mass_total_after, scalars = perform_numbers(
         (
             mass_before,
             mass_after,
@@ -215,8 +219,7 @@
                     aggregate_regridded,
                 ]
             ),
-        ),
-        ("gx", "gy"),
+        )
     )
     enthalpy_global_preceding = scalars[0]
     enthalpy_global_following = scalars[1]

time: 96.3 us -> 82.4 us (0.86)
  blocking collectives: 39.4 us -> 24.7 us
    psum x1 -> x2, blocking collectives: 39.4 us -> 24.7 us  [perform_numbers(): return lax.psum(lax.psum(block_in, 'gx'), axis_name='gy')]
  transfers between devices with their start and end apart: 4 -> 4, of which waited for: 1 -> 1; matrix products, arithmetic and copies ran while one was open for 28% -> 34% of each run, Pallas kernels for 0% -> 0%
where the time goes in v1:
time: 82.4 us; the launch traced here: 81.8 us
  other arithmetic  26.3 us (32%)
  blocking collectives  24.7 us (30%)
  local copies, waits for them, and re-layouts  15.3 us (19%)
  between operations  8.13 us (10%)
  starting transfers between devices  7.19 us (9%)
    psum x2, blocking collectives, perform_numbers(): return lax.psum(lax.psum(block_in, 'gx'), axis_name='gy')  24.7 us
    reduce_sum x1, other arithmetic, local(): mass_after = jnp.sum(tracer_new * regridded_depths, axis=(1, 2, 3))  7.75 us
    ppermute x4, starting transfers between devices, passed_along(): return lax.ppermute(value, axis, pairs)  7.19 us
    reduce_sum x1, other arithmetic, local(): jnp.sum(0.5 * (regridded_depths + jnp.concatenate([regridded_depths[:, :,...  3.61 us
    slice x14, local copies, waits for them, and re-layouts, shifted_layers(): return jnp.concatenate([filler, values[..., :layers + amount, :]], axis=-2)  2.65 us
    unnamed x33, local copies, waits for them, and re-layouts  2.59 us
    div x2, other arithmetic, multiply_by_regrid_operator(): (weight_first * mean_first + weight_second * mean_second) / (weight_first...  2 us
    concatenate x12, other arithmetic, ppm_parts(): jnp.concatenate([top_edge, second_edge, inner_edge, lower_edge, bottom_ed...  1.73 us
  transfers between devices with their start and end apart: 4, of which 1 were waited for; matrix products, arithmetic and copies ran while one was open for 34% of the time, Pallas kernels for 0%

profile of v1, /device:TPU:0, one launch (start us, length us, event | category | flops | bytes accessed | tf_op | source)
XLA Modules:
  0.0 81.8 jit_solution(8116940391586543152)
XLA Ops:
  0.6 1.7 %slice.551 = f32[2,120,1]{2,1,0:T(8,128)} slice(f32[2,120,128]{2,1,0:T(8,128)} %param.10), slice={[0:2], [0:120], [127:128]} | slice | bytes 1920 | tf_op jit(solution)/shard_map/slice | solution.py:169
  2.3 3.0 %collective-permute-start.2 = (f32[2,120,1]{2,1,0:T(8,128)}, f32[2,120,1]{2,1,0:T(8,128)}, u32[]{:S(2)}, u32[]{:S(2)}) collective-permute-start(f32[2,120,1]{2,1,0:T(8,128)} %slice.551), channel_id=1, source_target_pairs={{0,8},{8,16},{16,24},{24,0},{1,9},{9,17},{17,25},{25,1},{2,10},{10... | collective-permute-start | bytes 2888 | tf_op jit(solution)/shard_map/ppermute | solution.py:13
  6.0 1.0 %copy-done.2 = bf16[8,2,120,128]{3,2,1,0:T(8,128)(2,1)S(1)} copy-done((bf16[8,2,120,128]{3,2,1,0:T(8,128)(2,1)S(1)}, bf16[8,2,120,128]{3,2,1,0:T(8,128)(2,1)}, u32[]{:S(2)}) %copy-start.2) | copy-done | bytes 491544
  9.2 0.8 copy-done.1
  10.0 0.7 fusion.46
  12.6 0.7 fusion.61
  13.2 0.8 fusion.98
  14.0 0.8 fusion.99
  14.8 0.7 fusion.40
  16.2 7.7 %multiply_reduce_fusion = (f32[8]{0:T(128)S(1)}, f32[8,2,120,128]{3,2,1,0:T(8,128)S(1)}) fusion(f32[2,120,128]{2,1,0:T(8,128)S(1)} %get-tuple-element.128, f32[2,120,128]{2,1,0:T(8,128)S(1)} %get-tuple-element.144, f32[2,120,128]{2,1,0:T(8,128)S(1)} %get-tuple-element.143, pred[2,120,128]{2,1,0:T(8,128)(4,1)S(1)} %get-tuple-element.130, ...), kind=kLoop, calls=%fused_computation.18 | loop fusion | flops 24084472 | bytes 17244192 | tf_op jit(solution)/shard_map/reduce_sum | solution.py:204
  23.9 0.7 slice.715
  24.7 0.7 slice.709
  25.3 0.7 slice.704
  27.3 1.0 %maximum_bitcast_fusion.1 = f32[1,2,120,128]{3,2,1,0:T(8,128)S(1)} fusion(f32[2,120,127]{2,1,0:T(8,128)S(1)} %get-tuple-element.109, f32[2,120,1]{2,1,0:T(8,128)} %collective-permute-done.2), kind=kLoop, calls=%fused_computation.153 | loop fusion | flops 30720 | bytes 245760 | tf_op jit(solution)/shard_map/stack | solution.py:172
  28.8 1.0 %add_divide_fusion.1 = f32[2,2,120,128]{3,2,1,0:T(8,128)S(1)} fusion(f32[2,2,120,128]{3,2,1,0:T(8,128)S(1)} %get-tuple-element.74, f32[2,2,117,128]{3,2,1,0:T(8,128)S(1)} %slice.692, f32[2,2,118,128]{3,2,1,0:T(8,128)S(1)} %get-tuple-element.93, f32[2,2,119,128]{3,2,1,0:T(8,128)S(1)} %get-tuple-element.95, f32[2,2,119,128]{3,2,1,0:T(8,128)S(1)} %get-tuple-element.94, ...), kind=kLoop, calls=%fused_computation.105 | loop fusion | flops 5591040 | bytes 5355520 | tf_op jit(solution)/shard_map/div | solution.py:103
  30.0 0.8 slice.718
  30.7 1.2 %collective-permute-start.3 = (f32[3,2,120,1]{2,1,3,0:T(2,128)S(1)}, f32[3,2,120,1]{2,1,3,0:T(2,128)S(1)}, u32[]{:S(2)}, u32[]{:S(2)}) collective-permute-start(f32[3,2,120,1]{2,1,3,0:T(2,128)S(1)} %pad_maximum_fusion.23), channel_id=1, source_target_pairs={{0,24},{8,0},{16,8},{24,16},{1,25},{9,1},{17,9},{25,17},{2,26},{10... | collective-permute-start | bytes 8648 | tf_op jit(solution)/shard_map/ppermute | solution.py:13
  32.0 0.8 %maximum_bitcast_fusion = f32[1,2,120,128]{3,2,1,0:T(8,128)S(1)} fusion(f32[1,120,128]{2,1,0:T(8,128)S(1)} %get-tuple-element.121, f32[1,120,128]{2,1,0:T(8,128)} %collective-permute-done), kind=kLoop, calls=%fused_computation.152 | loop fusion | flops 30720 | bytes 245760 | tf_op jit(solution)/shard_map/stack | solution.py:147
  33.4 1.0 %add_divide_fusion.2 = f32[2,2,120,128]{3,2,1,0:T(8,128)S(1)} fusion(f32[2,2,120,128]{3,2,1,0:T(8,128)S(1)} %get-tuple-element.72, f32[2,2,117,128]{3,2,1,0:T(8,128)S(1)} %slice.660, f32[2,2,118,128]{3,2,1,0:T(8,128)S(1)} %get-tuple-element.82, f32[2,2,119,128]{3,2,1,0:T(8,128)S(1)} %get-tuple-element.84, f32[2,2,119,128]{3,2,1,0:T(8,128)S(1)} %get-tuple-element.83, ...), kind=kLoop, calls=%fused_computation.106 | loop fusion | flops 5591040 | bytes 5355520 | tf_op jit(solution)/shard_map/div | solution.py:103
  35.2 0.7 pad_maximum_fusion.17
  35.9 3.0 %collective-permute-start.1 = (f32[3,1,120,128]{3,2,1,0:T(8,128)}, f32[3,1,120,128]{3,2,1,0:T(8,128)}, u32[]{:S(2)}, u32[]{:S(2)}) collective-permute-start(f32[3,1,120,128]{3,2,1,0:T(8,128)} %pad_maximum_fusion.17), channel_id=1, source_target_pairs={{0,7},{1,0},{2,1},{3,2},{4,3},{5,4},{6,5},{7,6},{8,15},{9,8},{10,9... | collective-permute-start | bytes 552968 | tf_op jit(solution)/shard_map/ppermute | solution.py:13
  38.9 0.8 copy.187
  39.7 0.8 copy.188
  40.6 0.8 fusion.47
  42.3 0.9 %slice_bitcast_fusion.3 = (f32[1,120,128]{2,1,0:T(8,128)S(1)}, f32[1,120,128]{2,1,0:T(8,128)S(1)}) fusion(f32[3,1,120,128]{3,2,1,0:T(8,128)} %collective-permute-done.1), kind=kLoop, calls=%fused_computation.177 | loop fusion | bytes 245760 | tf_op jit(solution)/shard_map/squeeze | solution.py:162
  43.2 3.6 %fusion.49 = (f32[]{:T(128)}, f32[]{:T(128)}, f32[]{:T(128)}, f32[]{:T(128)}, f32[2,120,128]{2,1,0:T(8,128)}, /*index=5*/f32[2,120,128]{2,1,0:T(8,128)}, f32[2,120,128]{2,1,0:T(8,128)}) fusion(f32[2,120,128]{2,1,0:T(8,128)S(1)} %get-tuple-element.128, f32[2,120,1]{2,1,0:T(8,128)} %copy.187, f32[2,120,127]{2,1,0:T(8,128)} %slice.715, ...), kind=kLoop, calls=%fused_computation.136 | loop fusion | flops 3839996 | bytes 3906576 | tf_op jit(solution)/shard_map/reduce_sum | solution.py:194
  48.6 1.5 %fusion.63 = (f32[]{:T(128)}, f32[]{:T(128)}) fusion(f32[3,1,120,128]{3,2,1,0:T(8,128)} %collective-permute-done.1, f32[2,120,128]{2,1,0:T(8,128)S(1)} %copy-done, f32[2,120,128]{2,1,0:T(8,128)S(1)} %copy-done.4), kind=kLoop, calls=%fused_computation.176 | loop fusion | flops 153598 | bytes 307208 | tf_op jit(solution)/shard_map/reduce_sum | solution.py:156
  51.4 0.7 pad_maximum_fusion.24
  52.1 9.5 %all-reduce.66 = (f32[8]{0:T(128)S(1)}, f32[8]{0:T(128)S(1)}, f32[3]{0:T(128)S(1)}) all-reduce(f32[8]{0:T(128)S(1)} %get-tuple-element.70, f32[8]{0:T(128)S(1)} %get-tuple-element.39, f32[3]{0:T(128)S(1)} %pad_maximum_fusion.24), channel_id=1, replica_groups=mesh['gx'=4,'gy'=8] {'gx'}, use_global_device_ids=true, to_apply=%region_1.2 | all-reduce | flops 19 | bytes 152 | tf_op jit(solution)/shard_map/psum | solution.py:120
  61.5 15.3 %all-reduce.65 = (f32[8]{0:T(128)S(1)}, f32[8]{0:T(128)S(1)}, f32[3]{0:T(128)S(1)}) all-reduce(f32[8]{0:T(128)S(1)} %get-tuple-element.21, f32[8]{0:T(128)S(1)} %get-tuple-element.22, f32[3]{0:T(128)S(1)} %get-tuple-element.23), channel_id=1, replica_groups=mesh['gx'=4,'gy'=8] {'gy'}, use_global_device_ids=true, to_apply=%region_2.3 | all-reduce | flops 19 | bytes 152 | tf_op jit(solution)/shard_map/psum | solution.py:120
  78.7 1.1 %broadcast_add_fusion = f32[8,2,120,128]{3,2,1,0:T(8,128)} fusion(f32[8,2,120,128]{3,2,1,0:T(8,128)S(1)} %get-tuple-element.40, f32[8]{0:T(128)S(1)} %subtract_divide_fusion), kind=kLoop, calls=%fused_computation.57 | loop fusion | flops 245760 | bytes 1966112 | tf_op jit(solution)/shard_map/add | solution.py:228
  81.1 0.7 broadcast_add_fusion.1
  (95 shorter events, 8.8 us)
Async XLA Ops:
  0.6 4.7 %copy-start.4 = (f32[2,120,128]{2,1,0:T(8,128)S(1)}, f32[2,120,128]{2,1,0:T(8,128)}, u32[]{:S(2)}) copy-start(f32[2,120,128]{2,1,0:T(8,128)} %param.9) | copy-start | bytes 368644
  2.3 3.6 %copy-start = (f32[2,120,128]{2,1,0:T(8,128)S(1)}, f32[2,120,128]{2,1,0:T(8,128)}, u32[]{:S(2)}) copy-start(f32[2,120,128]{2,1,0:T(8,128)} %param.12) | copy-start | bytes 368644
  2.3 24.9 %collective-permute-start.2 = (f32[2,120,1]{2,1,0:T(8,128)}, f32[2,120,1]{2,1,0:T(8,128)}, u32[]{:S(2)}, u32[]{:S(2)}) collective-permute-start(f32[2,120,1]{2,1,0:T(8,128)} %slice.551), channel_id=1, source_target_pairs={{0,8},{8,16},{16,24},{24,0},{1,9},{9,17},{17,25},{25,1},{2,10},{10... | collective-permute-start | bytes 2888 | tf_op jit(solution)/shard_map/ppermute | solution.py:13
  5.9 26.0 %collective-permute-start = (f32[1,120,128]{2,1,0:T(8,128)}, f32[1,120,128]{2,1,0:T(8,128)}, u32[]{:S(2)}, u32[]{:S(2)}) collective-permute-start(f32[1,120,128]{2,1,0:T(8,128)} %get-tuple-element.120), channel_id=1, source_target_pairs={{0,1},{1,2},{2,3},{3,4},{4,5},{5,6},{6,7},{7,0},{8,9},{9,10},{10,1... | collective-permute-start | bytes 184328 | tf_op jit(solution)/shard_map/ppermute | solution.py:13
  6.0 1.0 %copy-start.2 = (bf16[8,2,120,128]{3,2,1,0:T(8,128)(2,1)S(1)}, bf16[8,2,120,128]{3,2,1,0:T(8,128)(2,1)}, u32[]{:S(2)}) copy-start(bf16[8,2,120,128]{3,2,1,0:T(8,128)(2,1)} %param.8) | copy-start | bytes 1474564
  9.1 0.9 %copy-start.1 = (f32[2,120,128]{2,1,0:T(8,128)S(1)}, f32[2,120,128]{2,1,0:T(8,128)}, u32[]{:S(2)}) copy-start(f32[2,120,128]{2,1,0:T(8,128)} %param.10) | copy-start | bytes 368644
  10.0 0.8 %copy-start.12 = (bf16[2,120,128]{2,1,0:T(8,128)(2,1)S(1)}, bf16[2,120,128]{2,1,0:T(8,128)(2,1)}, u32[]{:S(2)}) copy-start(bf16[2,120,128]{2,1,0:T(8,128)(2,1)} %param.14) | copy-start | bytes 184324
  10.0 0.9 %copy-start.13 = (bf16[2,120,128]{2,1,0:T(8,128)(2,1)S(1)}, bf16[2,120,128]{2,1,0:T(8,128)(2,1)}, u32[]{:S(2)}) copy-start(bf16[2,120,128]{2,1,0:T(8,128)(2,1)} %param.15) | copy-start | bytes 184324
  10.0 1.0 %copy-start.15 = (s32[2,120,128]{2,1,0:T(8,128)S(1)}, s32[2,120,128]{2,1,0:T(8,128)}, u32[]{:S(2)}) copy-start(s32[2,120,128]{2,1,0:T(8,128)} %param.13) | copy-start | bytes 368644
  11.5 1.0 %copy-start.3 = (f32[2,120,128]{2,1,0:T(8,128)S(1)}, f32[2,120,128]{2,1,0:T(8,128)}, u32[]{:S(2)}) copy-start(f32[2,120,128]{2,1,0:T(8,128)} %param.11) | copy-start | bytes 368644
  30.7 8.2 %collective-permute-start.3 = (f32[3,2,120,1]{2,1,3,0:T(2,128)S(1)}, f32[3,2,120,1]{2,1,3,0:T(2,128)S(1)}, u32[]{:S(2)}, u32[]{:S(2)}) collective-permute-start(f32[3,2,120,1]{2,1,3,0:T(2,128)S(1)} %pad_maximum_fusion.23), channel_id=1, source_target_pairs={{0,24},{8,0},{16,8},{24,16},{1,25},{9,1},{17,9},{25,17},{2,26},{10... | collective-permute-start | bytes 8648 | tf_op jit(solution)/shard_map/ppermute | solution.py:13
  34.4 0.8 %copy-start.11 = (f32[1,1,120,128]{3,2,1,0:T(8,128)S(1)}, f32[1,1,120,128]{3,2,1,0:T(8,128)}, u32[]{:S(2)}) copy-start(f32[1,1,120,128]{3,2,1,0:T(8,128)} %get-tuple-element.119) | copy-start | bytes 184324
  35.9 6.4 %collective-permute-start.1 = (f32[3,1,120,128]{3,2,1,0:T(8,128)}, f32[3,1,120,128]{3,2,1,0:T(8,128)}, u32[]{:S(2)}, u32[]{:S(2)}) collective-permute-start(f32[3,1,120,128]{3,2,1,0:T(8,128)} %pad_maximum_fusion.17), channel_id=1, source_target_pairs={{0,7},{1,0},{2,1},{3,2},{4,3},{5,4},{6,5},{7,6},{8,15},{9,8},{10,9... | collective-permute-start | bytes 552968 | tf_op jit(solution)/shard_map/ppermute | solution.py:13
  39.7 3.4 %copy-start.7 = (f32[2,118,128]{2,1,0:T(8,128)S(1)}, f32[2,118,128]{2,1,0:T(8,128)}, u32[]{:S(2)}) copy-start(f32[2,118,128]{2,1,0:T(8,128)} %get-tuple-element.159) | copy-start | bytes 362500
  39.7 3.5 %copy-start.8 = (f32[2,118,128]{2,1,0:T(8,128)S(1)}, f32[2,118,128]{2,1,0:T(8,128)}, u32[]{:S(2)}) copy-start(f32[2,118,128]{2,1,0:T(8,128)} %get-tuple-element.160) | copy-start | bytes 362500
  39.7 3.5 %copy-start.14 = (f32[1,120,128]{2,1,0:T(8,128)S(1)}, f32[1,120,128]{2,1,0:T(8,128)}, u32[]{:S(2)}) copy-start(f32[1,120,128]{2,1,0:T(8,128)} %get-tuple-element.118) | copy-start | bytes 184324
  40.5 2.7 %copy-start.9 = (f32[2,119,128]{2,1,0:T(8,128)S(1)}, f32[2,119,128]{2,1,0:T(8,128)}, u32[]{:S(2)}) copy-start(f32[2,119,128]{2,1,0:T(8,128)} %get-tuple-element.112) | copy-start | bytes 365572
  42.1 1.1 %copy-start.5 = (f32[2,118,128]{2,1,0:T(8,128)S(1)}, f32[2,118,128]{2,1,0:T(8,128)}, u32[]{:S(2)}) copy-start(f32[2,118,128]{2,1,0:T(8,128)} %get-tuple-element.110) | copy-start | bytes 362500
  42.1 1.1 %copy-start.6 = (f32[2,118,128]{2,1,0:T(8,128)S(1)}, f32[2,118,128]{2,1,0:T(8,128)}, u32[]{:S(2)}) copy-start(f32[2,118,128]{2,1,0:T(8,128)} %get-tuple-element.111) | copy-start | bytes 362500
  78.7 2.4 %copy-start.10 = (f32[2,120,128]{2,1,0:T(8,128)S(1)}, f32[2,120,128]{2,1,0:T(8,128)}, u32[]{:S(2)}) copy-start(f32[2,120,128]{2,1,0:T(8,128)} %get-tuple-element.24) | copy-start | bytes 368644
